TPU v7x, 16 devices: a whole 2x2x2 slice. The times are simulated.
16 devices in a mesh: rep: 1, dp: 16 (over x, y, z, core).
Axes of the slice: x: 2, y: 2, z: 2, core: 2. Of those that a mesh axis runs over, the one named last changes fastest.
Arguments:
- g_w_gate: bfloat16 [16, 2, 1280, 4480], P(('rep', 'dp'))
- g_w_up: bfloat16 [16, 2, 1280, 4480], P(('rep', 'dp'))
- g_w_down: bfloat16 [16, 2, 4480, 1280], P(('rep', 'dp'))
- w_gate: bfloat16 [2, 1280, 4480], replicated
- w_up: bfloat16 [2, 1280, 4480], replicated
- w_down: bfloat16 [2, 4480, 1280], replicated
- m_w_gate: float32 [2, 1280, 4480], P(None, 'dp')
- m_w_up: float32 [2, 1280, 4480], P(None, 'dp')
- m_w_down: float32 [2, 4480, 1280], P(None, 'dp')
- v_w_gate: float32 [2, 1280, 4480], P(None, 'dp')
- v_w_up: float32 [2, 1280, 4480], P(None, 'dp')
- v_w_down: float32 [2, 4480, 1280], P(None, 'dp')
Outputs:
- output 1: bfloat16 [2, 1280, 4480], P('rep')
- output 2: bfloat16 [2, 1280, 4480], P('rep')
- output 3: bfloat16 [2, 4480, 1280], P('rep')
- output 4: float32 [2, 1280, 4480], P('rep', 'dp')
- output 5: float32 [2, 1280, 4480], P('rep', 'dp')
- output 6: float32 [2, 4480, 1280], P('rep', 'dp')
- output 7: float32 [2, 1280, 4480], P('rep', 'dp')
- output 8: float32 [2, 1280, 4480], P('rep', 'dp')
- output 9: float32 [2, 4480, 1280], P('rep', 'dp')
All inputs are finite; a program needn't handle non-finite values.
Results may differ from a plain program's by a relative error of at most 0.022.
Values are sent between devices in bfloat16 or wider.
A program may use at most 2 GiB of HBM per device.

v0:
```python
import jax
import jax.numpy as jnp
from jax import lax
from jax.sharding import PartitionSpec as P


def adamw(w, m, v, g):
    m = 0.9 * m + 0.1 * g
    v = 0.95 * v + 0.05 * g * g
    step = m * lax.rsqrt(v + 1e-8) + 0.1 * w
    return (w - 0.02 * step).astype(jnp.bfloat16), m, v


def solution(mesh):
    def step(*arrays):
        terms, weights, m, v = (arrays[i : i + 3] for i in (0, 3, 6, 9))
        gradients = [lax.psum_scatter(t[0], "dp", scatter_dimension=1, tiled=True).astype(jnp.float32) for t in terms]
        me = lax.axis_index("dp")
        own = [lax.dynamic_slice_in_dim(w, me * one.shape[1], one.shape[1], 1).astype(jnp.float32) for w, one in zip(weights, m, strict=True)]
        new = [adamw(w, m, v, g) for w, m, v, g in zip(own, m, v, gradients, strict=True)]
        whole = [lax.all_gather(one[0], "dp", axis=1, tiled=True) for one in new]
        return (*whole, *(one[1] for one in new), *(one[2] for one in new))

    all_of, cut = P(None, None, None), P(None, "dp", None)
    return jax.shard_map(
        step,
        mesh=mesh,
        in_specs=(P(("rep", "dp"), None, None, None),) * 3 + (all_of,) * 3 + (cut,) * 6,
        out_specs=(P("rep", None, None),) * 3 + (P("rep", "dp", None),) * 6,
        check_vma=False,
    )
```

profile of v0, /device:TPU:0, one launch (start us, length us, event | category | flops | bytes accessed | tf_op | source)
XLA Modules:
  0.0 1086.7 jit_solution(14518706993465798221)
XLA Ops:
  7.2 0.0 reduce-scatter.8.cloned.1.call-start
  7.2 0.7 reduce-scatter.8.cloned.1.call-update
  7.9 0.0 reduce-scatter.6.cloned.1.call-start
  8.0 0.7 reduce-scatter.6.cloned.1.call-update
  8.7 0.0 reduce-scatter.10.cloned.1.call-start
  8.7 104.8 %copy.21 = bf16[2,4480,1280]{2,0,1:T(2,128)(2,1)S(1)} copy(bf16[2,4480,1280]{2,1,0:T(8,128)(2,1)} %bitcast.9) | data formatting | bytes 45875200
  113.5 8.2 copy.23
  121.6 0.0 copy-start.1
  121.6 0.0 reduce-scatter.10.cloned.1.call-update
  121.7 0.0 all-gather.6.cloned.1.call-start
  121.7 123.6 %reduce-scatter.8.cloned.1.call-done = bf16[2,80,4480]{2,1,0:T(8,128)(2,1)} async-done(((bf16[2,1280,4480]{2,1,0:T(8,128)(2,1)}), bf16[2,80,4480]{2,1,0:T(8,128)(2,1)}) %reduce-scatter.8.cloned.1.call-update) | async-done | bytes 1433616 | tf_op jit(solution)/shard_map/reduce_scatter | solution.py:17
  245.3 0.0 copy-done.1
  245.3 6.4 fusion.6
  251.7 0.0 all-gather.6.cloned.1.call-update
  251.7 0.0 all-gather.4.cloned.1.call-start
  251.8 234.0 %reduce-scatter.6.cloned.1.call-done = bf16[2,80,4480]{2,1,0:T(8,128)(2,1)} async-done(((bf16[2,1280,4480]{2,1,0:T(8,128)(2,1)}), bf16[2,80,4480]{2,1,0:T(8,128)(2,1)}) %reduce-scatter.6.cloned.1.call-update) | async-done | bytes 1433616 | tf_op jit(solution)/shard_map/reduce_scatter | solution.py:17
  485.7 7.2 fusion.2
  493.0 0.0 all-gather.4.cloned.1.call-update
  493.0 0.0 all-gather.8.cloned.1.call-start
  493.0 233.7 %reduce-scatter.10.cloned.1.call-done = bf16[280,2560]{1,0:T(8,128)(2,1)} async-done(((bf16[4480,2560]{1,0:T(8,128)(2,1)}), bf16[280,2560]{1,0:T(8,128)(2,1)}) %reduce-scatter.10.cloned.1.call-update) | async-done | bytes 1433616
  726.7 3.4 reshape.19
  730.1 6.9 fusion.10
  737.0 0.0 all-gather.8.cloned.1.call-update
  737.0 94.5 %all-gather.6.cloned.1.call-done = bf16[2,1280,4480]{2,1,0:T(8,128)(2,1)} async-done(((bf16[2,80,4480]{2,1,0:T(8,128)(2,1)}), bf16[2,1280,4480]{2,1,0:T(8,128)(2,1)}) %all-gather.6.cloned.1.call-update) | async-done | bytes 22937616 | tf_op jit(solution)/shard_map/all_gather | solution.py:21
  831.5 98.9 %all-gather.4.cloned.1.call-done = bf16[2,1280,4480]{2,1,0:T(8,128)(2,1)} async-done(((bf16[2,80,4480]{2,1,0:T(8,128)(2,1)}), bf16[2,1280,4480]{2,1,0:T(8,128)(2,1)}) %all-gather.4.cloned.1.call-update) | async-done | bytes 22937616 | tf_op jit(solution)/shard_map/all_gather | solution.py:21
  930.4 98.9 %all-gather.8.cloned.1.call-done = bf16[2,4480,1280]{2,1,0:T(8,128)(2,1)} async-done(((bf16[2,280,1280]{2,1,0:T(8,128)(2,1)}), bf16[2,4480,1280]{2,1,0:T(8,128)(2,1)}) %all-gather.8.cloned.1.call-update) | async-done | bytes 22937616 | tf_op jit(solution)/shard_map/all_gather | solution.py:21
  1029.4 0.0 copy-start
  1029.4 15.8 %copy.31 = bf16[2,1280,4480]{2,1,0:T(8,128)(2,1)} copy(bf16[2,1280,4480]{2,1,0:T(8,128)(2,1)} %all-gather.4.cloned.1.call-done) | data formatting | bytes 45875200
  1045.2 6.7 copy-done
  1051.9 8.2 copy.32
  1060.1 19.8 %copy.33 = bf16[2,4480,1280]{2,1,0:T(8,128)(2,1)} copy(bf16[2,4480,1280]{2,1,0:T(8,128)(2,1)} %all-gather.8.cloned.1.call-done) | data formatting | bytes 45875200
Async XLA Ops:
  7.2 238.1 %reduce-scatter.8.cloned.1.call-start = ((), (), s32[]{:S(2)}) async-start(), calls=%async_computation.5 | async-start | bytes 24371200 | tf_op jit(solution)/shard_map/reduce_scatter | solution.py:17
  7.9 477.8 %reduce-scatter.6.cloned.1.call-start = ((), (), s32[]{:S(2)}) async-start(), calls=%async_computation.3 | async-start | bytes 24371200 | tf_op jit(solution)/shard_map/reduce_scatter | solution.py:17
  8.7 718.0 %reduce-scatter.10.cloned.1.call-start = ((), (), s32[]{:S(2)}) async-start(), calls=%async_computation.8 | async-start | bytes 24371200
  121.6 123.6 %copy-start.1 = (f32[2,80,4480]{2,1,0:T(8,128)S(1)}, f32[2,80,4480]{2,1,0:T(8,128)}, u32[]{:S(2)}) copy-start(f32[2,80,4480]{2,1,0:T(8,128)} %param.22) | copy-start | bytes 8601604
  121.7 709.9 %all-gather.6.cloned.1.call-start = ((), (), s32[]{:S(2)}) async-start(), calls=%async_computation.6 | async-start | bytes 24371200 | tf_op jit(solution)/shard_map/all_gather | solution.py:21
  251.7 678.7 %all-gather.4.cloned.1.call-start = ((), (), s32[]{:S(2)}) async-start(), calls=%async_computation.4 | async-start | bytes 24371200 | tf_op jit(solution)/shard_map/all_gather | solution.py:21
  493.0 536.4 %all-gather.8.cloned.1.call-start = ((), (), s32[]{:S(2)}) async-start(), calls=%async_computation.7 | async-start | bytes 24371200 | tf_op jit(solution)/shard_map/all_gather | solution.py:21
  1029.4 22.5 %copy-start = (bf16[2,1280,4480]{2,1,0:T(8,128)(2,1)S(1)}, bf16[2,1280,4480]{2,1,0:T(8,128)(2,1)}, u32[]{:S(2)}) copy-start(bf16[2,1280,4480]{2,1,0:T(8,128)(2,1)} %all-gather.6.cloned.1.call-done) | copy-start | bytes 68812800
Sparse Core Ops, SparseCore 0:
  10.3 234.9 reduce-scatter.7
  247.6 238.0 reduce-scatter.5
  488.6 238.0 reduce-scatter.9
  729.4 102.0 all-gather.5
  834.2 96.1 all-gather.3
  933.1 96.1 all-gather.7
where the time goes:
time: 1090 us
  waiting for transfers between devices  885 us (81%)
  local copies, waits for them, and re-layouts  167 us (15%)
  other arithmetic  20.5 us (2%)
  between operations  14.1 us (1%)
    reduce_scatter x2, waiting for transfers between devices, step(): lax.psum_scatter(t[0], 'dp', scatter_dimension=1, tiled=True)  358 us
    all_gather x3, waiting for transfers between devices, step(): whole = [lax.all_gather(one[0], 'dp', axis=1, tiled=True) for one in new]  292 us
    unnamed x7, waiting for transfers between devices  235 us
    unnamed x10, local copies, waits for them, and re-layouts  167 us
  transfers between devices with their start and end apart: 6, of which 6 were waited for; matrix products, arithmetic and copies ran while one was open for 13% of the time, Pallas kernels for 0%

commit v1 on v0

v1 whole, which is shorter than its diff:
```python
import jax
import jax.numpy as jnp
from jax import lax
from jax.experimental import pallas as pl
from jax.experimental.pallas import tpu as pltpu
from jax.sharding import PartitionSpec as P

MESH = pl.DeviceIdType.MESH
BITS = (4, 2, 1)
AXES = 3


def order(stream):
    return tuple(BITS[(stream + i) % AXES] for i in range(AXES))


def halving(stream):
    a, b, c = order(stream)
    return {1: (a | b | c, a | b, a | c, a), 2: (b | c, b), 3: (c,), 4: (0,)}


def inputs_of(stream, step, r):
    a, b, c = order(stream)
    sub = (0, c, b, b | c)
    slots = [r]
    if step >= 2:
        slots.append(8 + sub.index(r))
    if step >= 3:
        slots.append(12 + (0, c).index(r))
    if step >= 4:
        slots.append(14)
    return slots


def lands_at(stream, step, r):
    a, b, c = order(stream)
    if step == 1:
        return 8 + (0, c, b, b | c).index(r ^ a)
    if step == 2:
        return 12 + (0, c).index(r ^ b)
    return 14


def plan():
    rs = lambda m, step, i: ("rs", m, step, i)
    ag = lambda m, axis, i: ("ag", m, axis, i)
    return (
        [rs(0, 1, i) for i in range(4)]
        + [rs(1, 1, 0), rs(0, 2, 0), rs(1, 1, 1), rs(0, 2, 1), rs(1, 1, 2)]
        + [rs(0, 3, 0), rs(1, 1, 3), rs(1, 2, 0), rs(1, 2, 1), rs(0, 4, 0)]
        + [ag(0, 0, 0), ag(0, 1, 0), ag(0, 2, 0), rs(1, 3, 0)]
        + [ag(0, 1, 1), ag(0, 2, 1), ag(0, 2, 2), ("c", 0, 0), rs(1, 4, 0)]
        + [ag(1, 0, 0), ag(1, 1, 0), ag(1, 2, 0), ag(0, 2, 3), ("c", 0, 1), ("c", 0, 2)]
        + [ag(1, 1, 1), ag(1, 2, 1), ("c", 1, 0), ag(1, 2, 2), ("c", 0, 3), ag(1, 2, 3)]
        + [("c", 1, 1), ("c", 1, 2), ("c", 1, 3)]
    )


AHEAD = 4


def kernel(*refs):
    g, w, m_in, v_in = (refs[i : i + 3] for i in (0, 3, 6, 9))
    out, m_out, v_out, land = (refs[i : i + 3] for i in (12, 15, 18, 21))
    stage, sent, m_buf, v_buf, w_buf, new = (refs[i : i + 3] for i in (24, 27, 30, 33, 36, 39))
    load_sem, state_sem, store_sem, cs_sem, cr_sem, rs_sem, rr_sem, as_sem, ar_sem, ds_sem, dr_sem = refs[42:]

    me = lax.axis_index("dp")
    chip, core = me // 2, me % 2
    partner = chip * 2 + (1 - core)

    def flip(bits):
        at = chip
        for bit in BITS:
            if bits & bit:
                at = at + bit - 2 * bit * ((at // bit) % 2)
        return at

    near = {bit: flip(bit) * 2 + core for bit in BITS}
    near[0] = partner

    barrier = pltpu.get_barrier_semaphore()
    for other in near.values():
        pl.semaphore_signal(barrier, inc=1, device_id={"dp": other}, device_id_type=MESH)
    pl.semaphore_wait(barrier, len(near))

    rows = [x.shape[1] for x in m_in]

    def block(s, r, of):
        return pl.ds(pl.multiple_of((flip(r) * 2 + of) * rows[s], 8), rows[s])

    def remote(src, dst, send, recv, to):
        return pltpu.make_async_remote_copy(
            src_ref=src, dst_ref=dst, send_sem=send, recv_sem=recv, device_id={"dp": to}, device_id_type=MESH
        )

    def cross(s, m, r):
        i = (s * 2 + m) * 8 + r
        return remote(g[s].at[0, m, block(s, r, 1 - core)], land[s].at[m, r], cs_sem.at[i], cr_sem.at[i], partner)

    def fall(s, m, step, r):
        slot = lands_at(s, step, r)
        i = (s * 2 + m) * 7 + slot - 8
        return remote(sent[s].at[m, slot - 8], land[s].at[m, slot], rs_sem.at[i], rr_sem.at[i], near[order(s)[step - 1]])

    def rise(s, m, axis, i):
        turn = order(s)
        known = (0, turn[0], turn[1], turn[0] | turn[1])[i]
        r = known | turn[axis]
        at = (s * 2 + m) * 7 + r - 1
        rows_of = block(s, known, core)
        src = new[s].at[m] if known == 0 else out[s].at[m, rows_of]
        return known, r, remote(src, out[s].at[m, rows_of], as_sem.at[at], ar_sem.at[at], near[turn[axis]])

    def over(s, m, r):
        i = (s * 2 + m) * 8 + r
        rows_of = block(s, r, core)
        src = new[s].at[m] if r == 0 else out[s].at[m, rows_of]
        return remote(src, out[s].at[m, rows_of], ds_sem.at[i], dr_sem.at[i], partner)

    def arrived(s, m, r):
        turn = order(s)
        last = max(axis for axis in range(AXES) if r & turn[axis])
        i = (0, turn[0], turn[1], turn[0] | turn[1]).index(r ^ turn[last])
        rise(s, m, last, i)[2].wait_recv()
        over(s, m, r).start()

    def state(s, m):
        pairs = ((m_in[s].at[m], m_buf[s]), (v_in[s].at[m], v_buf[s]), (w[s].at[m, block(s, 0, core)], w_buf[s]))
        return [pltpu.make_async_copy(src, dst, state_sem.at[s * 3 + i]) for i, (src, dst) in enumerate(pairs)]

    def store(s, m):
        pairs = ((m_buf[s], m_out[s].at[m]), (v_buf[s], v_out[s].at[m]), (new[s].at[m], out[s].at[m, block(s, 0, core)]))
        return [pltpu.make_async_copy(src, dst, store_sem.at[s * 3 + i]) for i, (src, dst) in enumerate(pairs)]

    def chunks(s, body):
        whole = rows[s] // 16

        @pl.loop(0, whole)
        def _(i):
            body(pl.ds(pl.multiple_of(i * 16, 16), 16))

        if rows[s] % 16:
            body(pl.ds(whole * 16, rows[s] % 16))

    def total(s, n, at):
        so_far = stage[s][0, at, :].astype(jnp.float32)
        for i in range(1, n):
            so_far = so_far + stage[s][i, at, :].astype(jnp.float32)
        return so_far

    def add(s, m, step, r, n):
        slot = lands_at(s, step, r) - 8

        def body(at):
            sent[s][m, slot, at, :] = total(s, n, at).astype(jnp.bfloat16)

        chunks(s, body)

    def adamw(s, m, n):
        def body(at):
            gradient = total(s, n, at).astype(jnp.bfloat16).astype(jnp.float32)
            w_old = w_buf[s][at, :].astype(jnp.float32)
            m_new = 0.9 * m_buf[s][at, :] + 0.1 * gradient
            v_new = 0.95 * v_buf[s][at, :] + 0.05 * gradient * gradient
            step = m_new * lax.rsqrt(v_new + 1e-8) + 0.1 * w_old
            m_buf[s][at, :] = m_new
            v_buf[s][at, :] = v_new
            new[s][m, at, :] = (w_old - 0.02 * step).astype(jnp.bfloat16)

        chunks(s, body)

    todo = plan()
    sums = [entry for entry in todo if entry[0] == "rs"]

    def send_cross(entry):
        _, m, step, i = entry
        for s in range(AXES):
            cross(s, m, halving(s)[step][i]).start()

    for entry in sums[:AHEAD]:
        send_cross(entry)
    for s in range(AXES):
        for copy in state(s, 0):
            copy.start()
    done = 0
    for entry in todo:
        if entry[0] == "rs":
            _, m, step, i = entry
            if done + AHEAD < len(sums):
                send_cross(sums[done + AHEAD])
            done += 1
            loads = []
            for s in range(AXES):
                r = halving(s)[step][i]
                slots = inputs_of(s, step, r)
                copies = [pltpu.make_async_copy(g[s].at[0, m, block(s, r, core)], stage[s].at[0], load_sem.at[s * 5])]
                for k, slot in enumerate(slots):
                    if slot < 8:
                        cross(s, m, slot).wait_recv()
                    else:
                        before = 1 if slot < 12 else 2 if slot < 14 else 3
                        turned = next(x for x in halving(s)[before] if lands_at(s, before, x) == slot)
                        fall(s, m, before, turned).wait_recv()
                    copies.append(pltpu.make_async_copy(land[s].at[m, slot], stage[s].at[k + 1], load_sem.at[s * 5 + k + 1]))
                for copy in copies:
                    copy.start()
                loads.append(copies)
            for s in range(AXES):
                r = halving(s)[step][i]
                for copy in loads[s]:
                    copy.wait()
                if step < 4:
                    add(s, m, step, r, len(loads[s]))
                    fall(s, m, step, r).start()
                else:
                    for copy in state(s, m):
                        copy.wait()
                    adamw(s, m, len(loads[s]))
                    over(s, m, 0).start()
                    for copy in store(s, m):
                        copy.start()
        elif entry[0] == "ag":
            _, m, axis, i = entry
            for s in range(AXES):
                known, _, copy = rise(s, m, axis, i)
                if i and axis == (1 if i == 1 else 2):
                    arrived(s, m, known)
                copy.start()
            if (m, axis, i) == (0, 2, 0):
                for s in range(AXES):
                    for copy in store(s, 0):
                        copy.wait()
                    for copy in state(s, 1):
                        copy.start()
        else:
            _, m, i = entry
            for s in range(AXES):
                turn = order(s)
                arrived(s, m, (0, turn[0], turn[1], turn[0] | turn[1])[i] | turn[2])

    for s in range(AXES):
        for copy in store(s, 1):
            copy.wait()
    for m in range(2):
        for s in range(AXES):
            for r in range(8):
                over(s, m, r).wait_recv()
                over(s, m, r).wait_send()
                cross(s, m, r).wait_send()
            for step in (1, 2, 3):
                for r in halving(s)[step]:
                    fall(s, m, step, r).wait_send()
            for axis in range(AXES):
                for i in range(2**axis):
                    rise(s, m, axis, i)[2].wait_send()


def solution(mesh):
    def step(*arrays):
        g, w, m, v = (arrays[i : i + 3] for i in (0, 3, 6, 9))
        layers = m[0].shape[0]
        blocks = [one.shape[1:] for one in m]
        shapes = (
            [jax.ShapeDtypeStruct(x.shape, x.dtype) for x in (*w, *m, *v)]
            + [jax.ShapeDtypeStruct((layers, 15, *b), jnp.bfloat16) for b in blocks]
        )
        anywhere = pl.BlockSpec(memory_space=pl.ANY)
        dma = pltpu.SemaphoreType.DMA
        result = pl.pallas_call(
            kernel,
            out_shape=shapes,
            in_specs=[anywhere] * 12,
            out_specs=[anywhere] * len(shapes),
            scratch_shapes=[
                *(pltpu.VMEM((5, *b), jnp.bfloat16) for b in blocks),
                *(pltpu.VMEM((layers, 7, *b), jnp.bfloat16) for b in blocks),
                *(pltpu.VMEM(b, jnp.float32) for b in blocks),
                *(pltpu.VMEM(b, jnp.float32) for b in blocks),
                *(pltpu.VMEM(b, jnp.bfloat16) for b in blocks),
                *(pltpu.VMEM((layers, *b), jnp.bfloat16) for b in blocks),
                dma((15,)),
                dma((9,)),
                dma((9,)),
                dma((48,)),
                dma((48,)),
                dma((42,)),
                dma((42,)),
                dma((42,)),
                dma((42,)),
                dma((48,)),
                dma((48,)),
            ],
            compiler_params=pltpu.CompilerParams(collective_id=0, has_side_effects=True, vmem_limit_bytes=67_000_000),
            name="sum_step_gather",
        )(*g, *w, *m, *v)
        return tuple(result[:9])

    all_of, cut = P(None, None, None), P(None, "dp", None)
    return jax.shard_map(
        step,
        mesh=mesh,
        in_specs=(P(("rep", "dp"), None, None, None),) * 3 + (all_of,) * 3 + (cut,) * 6,
        out_specs=(P("rep", None, None),) * 3 + (P("rep", "dp", None),) * 6,
        check_vma=False,
    )
```

time: 1090 us -> 513 us (0.47)
  waiting for transfers between devices: 885 us -> 0 us
  Pallas kernels: 0 us -> 449 us
  local copies, waits for them, and re-layouts: 167 us -> 62.1 us
  other arithmetic: 20.5 us -> 0.01 us
  between operations: 14.1 us -> 0.74 us
    pallas_call x0 -> x1, Pallas kernels: none -> 449 us  [step(): pl.pallas_call(kernel, out_shape=shapes, in_specs=[anywhere] * 12, out_sp...]
    reduce_scatter x2 -> x0, waiting for transfers between devices: 358 us -> none  [step(): lax.psum_scatter(t[0], 'dp', scatter_dimension=1, tiled=True)]
    all_gather x3 -> x0, waiting for transfers between devices: 292 us -> none  [step(): whole = [lax.all_gather(one[0], 'dp', axis=1, tiled=True) for one in new]]
    unnamed x7 -> x0, waiting for transfers between devices: 235 us -> none
    unnamed x10 -> x33, local copies, waits for them, and re-layouts: 167 us -> 62.1 us
    convert_element_type x3 -> x0, other arithmetic: 20.5 us -> none  [adamw(): return ((w - 0.02 * step).astype(jnp.bfloat16), m, v)]
  transfers between devices with their start and end apart: 6 -> 0, of which waited for: 6 -> 0; matrix products, arithmetic and copies ran while one was open for 13% -> 0% of each run, Pallas kernels for 0% -> 0%
where the time goes in v1:
time: 513 us; the launch traced here: 512 us
  Pallas kernels  449 us (88%)
  local copies, waits for them, and re-layouts  62.1 us (12%)
    pallas_call x1, Pallas kernels, step(): pl.pallas_call(kernel, out_shape=shapes, in_specs=[anywhere] * 12, out_sp...  449 us
    unnamed x33, local copies, waits for them, and re-layouts  62.1 us

profile of v1, /device:TPU:0, one launch (start us, length us, event | category | flops | bytes accessed | tf_op | source)
XLA Modules:
  0.0 511.9 jit_solution(4383218780524459109)
XLA Ops:
  0.6 449.1 %sum_step_gather.1 = (bf16[2,1280,4480]{2,1,0:T(8,128)(2,1)}, bf16[2,1280,4480]{2,1,0:T(8,128)(2,1)}, bf16[2,4480,1280]{2,1,0:T(8,128)(2,1)}, f32[2,80,4480]{2,1...) custom-call(bf16[1,2,1280,4480]{3,2,1,0:T(8,128)(2,1)} %refs_0_.1, ...), custom_call_target="tpu_custom_call" | custom-call | tf_op jit(solution)/shard_map/sum_step_gather/pallas_call | solution.py:270
  449.8 0.0 slice-start
  449.8 0.0 slice-start.1
  449.8 0.0 slice-start.2
  449.8 19.0 %copy.30 = bf16[2,1280,4480]{2,1,0:T(8,128)(2,1)} copy(bf16[2,1280,4480]{2,1,0:T(8,128)(2,1)} %get-tuple-element.36) | data formatting | bytes 45875200
  468.8 0.0 slice-start.3
  468.8 0.0 slice-start.4
  468.8 0.0 slice-start.5
  468.8 18.7 %copy.31 = bf16[2,1280,4480]{2,1,0:T(8,128)(2,1)} copy(bf16[2,1280,4480]{2,1,0:T(8,128)(2,1)} %get-tuple-element.37) | data formatting | bytes 45875200
  487.5 0.0 slice-done
  487.5 0.0 slice-done.1
  487.5 0.0 slice-done.2
  487.5 0.0 slice-done.3
  487.5 0.0 slice-done.4
  487.5 0.0 slice-done.5
  487.5 0.0 copy-start.5
  487.5 8.6 %copy.32 = bf16[2,4480,1280]{2,1,0:T(8,128)(2,1)} copy(bf16[2,4480,1280]{2,1,0:T(8,128)(2,1)S(1)} %bitcast.1) | data formatting | bytes 45875200
  496.1 0.0 copy-done.5
  496.1 0.0 copy-start.4
  496.1 1.6 copy.33
  497.7 1.3 copy-done.4
  499.0 0.0 copy-start.3
  499.0 1.6 copy.34
  500.6 1.3 copy-done.3
  501.8 0.0 copy-start.2
  501.8 1.6 copy.35
  503.4 1.3 copy-done.2
  504.7 0.0 copy-start.1
  504.7 1.6 copy.36
  506.2 1.3 copy-done.1
  507.5 0.0 copy-start
  507.5 1.6 copy.37
  509.1 1.3 copy-done
  510.4 1.6 copy.38
  (1 shorter events, 0.0 us)
Async XLA Ops:
  449.8 37.7 %slice-start = ((s8[22937600]{0:T(1024)(128)(4,1)}), s8[4194304]{0:T(1024)(128)(4,1)S(1)}, s32[]{:S(2)}) async-start(s8[22937600]{0:T(1024)(128)(4,1)} %bitcast), calls=%async_computation | async-start | bytes 8388608
  449.8 37.7 %slice-start.1 = ((s8[22937600]{0:T(1024)(128)(4,1)}), s8[4194304]{0:T(1024)(128)(4,1)S(1)}, s32[]{:S(2)}) async-start(s8[22937600]{0:T(1024)(128)(4,1)} %bitcast), calls=%async_computation.1 | async-start | bytes 8388608
  449.8 37.7 %slice-start.2 = ((s8[22937600]{0:T(1024)(128)(4,1)}), s8[4194304]{0:T(1024)(128)(4,1)S(1)}, s32[]{:S(2)}) async-start(s8[22937600]{0:T(1024)(128)(4,1)} %bitcast), calls=%async_computation.2 | async-start | bytes 8388608
  468.8 18.7 %slice-start.3 = ((s8[22937600]{0:T(1024)(128)(4,1)}), s8[4194304]{0:T(1024)(128)(4,1)S(1)}, s32[]{:S(2)}) async-start(s8[22937600]{0:T(1024)(128)(4,1)} %bitcast), calls=%async_computation.3 | async-start | bytes 8388608
  468.8 18.7 %slice-start.4 = ((s8[22937600]{0:T(1024)(128)(4,1)}), s8[4194304]{0:T(1024)(128)(4,1)S(1)}, s32[]{:S(2)}) async-start(s8[22937600]{0:T(1024)(128)(4,1)} %bitcast), calls=%async_computation.4 | async-start | bytes 8388608
  468.8 18.7 %slice-start.5 = ((s8[22937600]{0:T(1024)(128)(4,1)}), s8[1966080]{0:T(1024)(128)(4,1)S(1)}, s32[]{:S(2)}) async-start(s8[22937600]{0:T(1024)(128)(4,1)} %bitcast), calls=%async_computation.5 | async-start | bytes 3932160
  487.5 8.6 %copy-start.5 = (f32[2,80,4480]{2,1,0:T(8,128)S(1)}, f32[2,80,4480]{2,1,0:T(8,128)}, u32[]{:S(2)}) copy-start(f32[2,80,4480]{2,1,0:T(8,128)} %get-tuple-element.39) | copy-start | bytes 8601604
  496.1 2.8 copy-start.4
  499.0 2.8 copy-start.3
  501.8 2.8 copy-start.2
  504.7 2.8 copy-start.1
  507.5 2.8 copy-start
